TPU v7x, 32 devices: a whole 2x2x4 slice. The times are simulated.
32 devices in a mesh: term: 4 (over y, x), sector: 8 (over z, core).
Axes of the slice: x: 2, y: 2, z: 4, core: 2. Of those that a mesh axis runs over, the one named last changes fastest.
Arguments:
- wavefunction: float32 [8, 512, 512], P('sector'), may hold values from -120 to 120
- precond: float32 [8, 512, 512], P('sector', 'term'), may hold values from 0.05 to 4
- left_ops: float32 [8, 16, 512, 512], P('sector', 'term'), may hold values from -0.5 to 4.5
- right_ops: float32 [8, 16, 512, 512], P('sector', 'term'), may hold values from -1 to 2
- out_sector: int32 [8, 16], P('sector', 'term'), may hold values from 0 to 7, as said below
- live_counts: int32 [8, 4], P('sector', 'term'), may hold values from 1 to 4, as said below
Outputs:
- first_image: float32 [8, 512, 512], P('sector', 'term')
- correction: float32 [8, 512, 512], P('sector', 'term')
- second_image: float32 [8, 512, 512], P('sector', 'term')
Inputs may be any that keep to these rules, and one draw needn't show every extreme that they name: Each term moves the charge by at most one sector: out_sector[s, j] differs from s by at most 1. `live_counts`: in every sector some device has all 4 slots live.
All inputs are finite; a program needn't handle non-finite values.
Results may differ from a plain program's by a relative error of at most 0.0003.
Values sent between devices are 32-bit elements; how exact they have to be, the bound alone decides.
A program may use at most 64 MiB of HBM per device.

v0:
```python
import jax
import jax.numpy as jnp
from jax import lax
from jax.sharding import PartitionSpec as P


def from_behind(block, axis, distance):
    devices = range(lax.axis_size(axis))
    route = [(i - distance, i) for i in devices if i - distance in devices]
    return lax.ppermute(block, axis, route)


def matmul(first_op, second_op):
    return jnp.dot(
        first_op, second_op, precision=lax.Precision.HIGHEST, preferred_element_type=jnp.float32
    )


def term_rows(vector, left_stack, right_stack, offsets, kept, row_count):
    width = vector.shape[1]
    totals = jnp.zeros((row_count, 3, width), jnp.float32)

    def add_slot(slot_id, running):
        left_rows = left_stack[slot_id]
        product = matmul(matmul(left_rows, vector), right_stack[slot_id])
        return running.at[:, offsets[slot_id]].add(product)

    totals = lax.fori_loop(jnp.zeros((), jnp.int32), kept, add_slot, totals)
    return totals.reshape(row_count, 3 * width)


def per_device(wavefunction, precond, left_ops, right_ops, out_sector, live_counts):
    term_count = lax.axis_size("term")
    width = wavefunction.shape[1]
    slab_rows = width // term_count
    first_own = lax.axis_index("term") * slab_rows
    sector_id = lax.axis_index("sector")
    center = wavefunction[0]
    left_stack = left_ops[0]
    right_stack = right_ops[0]
    offsets = out_sector[0] - sector_id + 1
    count_here = live_counts[0, 0]

    def apply_hamiltonian(vector):
        whole = term_rows(vector, left_stack, right_stack, offsets, count_here, width).reshape(
            width, 3, width
        )
        upward = from_behind(whole[:, 2], "sector", 1)
        downward = from_behind(whole[:, 0], "sector", -1)
        return lax.psum_scatter(
            whole[:, 1] + upward + downward, "term", scatter_dimension=0, tiled=True
        )

    first_image = apply_hamiltonian(center)
    own_rows = lax.dynamic_slice_in_dim(center, first_own, slab_rows, 0)
    scaling = precond[0]
    cross, norm_sq = lax.psum(
        (jnp.sum(own_rows * first_image), jnp.sum(own_rows * own_rows)), ("term", "sector")
    )
    rayleigh = cross / norm_sq
    raw = scaling * (first_image - rayleigh * own_rows)
    correlation_sum = lax.psum(jnp.sum(own_rows * raw), ("term", "sector"))
    correction = raw - correlation_sum / norm_sq * own_rows
    full_correction = lax.all_gather(correction, "term", axis=0, tiled=True)
    second_image = apply_hamiltonian(full_correction)
    return (first_image[None], correction[None], second_image[None])


def solution(mesh):
    placed = (
        P("sector", None, None),
        P("sector", "term", None),
        P("sector", "term", None, None),
        P("sector", "term", None, None),
        P("sector", "term"),
        P("sector", "term"),
    )
    return jax.shard_map(
        per_device,
        mesh=mesh,
        in_specs=placed,
        out_specs=(P("sector", "term", None), P("sector", "term", None), P("sector", "term", None)),
        check_vma=False,
    )
```

profile of v0, /device:TPU:0, one launch (start us, length us, event | category | flops | bytes accessed | tf_op | source)
XLA Modules:
  0.0 316.2 jit_solution(16993770695380085301)
XLA Ops:
  7.2 0.0 copy-start.1
  7.2 0.0 reduce-scatter.3.cloned.1.call-start
  7.2 0.7 add_bitcast_fusion
  7.9 0.4 broadcast.48.clone
  8.3 0.0 copy-done.1
  8.3 11.7 %while.22 = (s32[]{:T(128)}, f32[512,3,512]{2,0,1:T(8,128)S(1)}, s32[]{:T(128)}, s32[4]{0:T(128)S(1)}, f32[4,512,512]{2,1,0:T(8,128)}, /*index=5*/f32[512,512]{1...) while((s32[]{:T(128)}, f32[512,3,512]{2,0,1:T(8,128)S(1)}, ...), condition=%wide.region_2.0_spmd, body=%wide.region_0.0_spmd.sunk | while | flops 3221749760 | bytes 7341298 | solution.py:28
  9.0 0.6 dynamic_slice.53
  11.5 0.7 and_reduce_fusion.4
  12.2 3.4 %fusion.44 = f32[512,512]{1,0:T(8,128)S(1)} fusion(f32[512,512]{1,0:T(8,128)} %get-tuple-element.260, f32[4,512,512]{2,1,0:T(8,128)} %get-tuple-element.259, s32[]{:T(128)S(6)} %select_n.28), kind=kOutput, calls=%fused_computation.4.clone.1 | convolution fusion | flops 1610612736 | bytes 3145732 | tf_op jit(solution)/shard_map/while/body/dot_general | solution.py:14
  15.6 3.8 %fusion.45 = f32[512,3,512]{2,0,1:T(8,128)S(1)} fusion(f32[512,3,512]{2,0,1:T(8,128)S(1)} %get-tuple-element.243, s32[]{:T(128)} %select_n.29, f32[512,512]{1,0:T(8,128)S(1)} %fusion.44, f32[4,512,512]{2,1,0:T(8,128)} %get-tuple-element.261, s32[]{:T(128)S(6)} %select_n.28, pred[]{:T(512)} %and_reduce_fusion.4), kind=kOutput, calls=%fused_computation.2.clone.1 | convolution fusion | flops 1611137024 | bytes 4195332 | tf_op jit(solution)/shard_map/while/body/dot_general | solution.py:14
  20.0 0.2 slice_bitcast_fusion.3
  20.2 0.0 copy-start
  20.2 2.6 collective-permute-start
  22.8 1.3 collective-permute-start.1
  24.1 0.9 collective-permute-done
  25.0 4.5 %collective-permute-done.1 = f32[512,512]{1,0:T(8,128)S(1)} collective-permute-done((f32[512,512]{1,0:T(8,128)S(1)}, f32[512,512]{1,0:T(8,128)S(1)}, u32[]{:S(2)}, u32[]{:S(2)}) %collective-permute-start.1) | collective-permute-done | bytes 1048608 | tf_op jit(solution)/shard_map/ppermute | solution.py:10
  29.5 1.4 fusion.17
  30.9 0.0 reduce-scatter.3.cloned.1.call-update
  30.9 0.0 all-gather.2.cloned.1.call-start
  30.9 72.2 %reduce-scatter.3.cloned.1.call-done = f32[128,512]{1,0:T(8,128)} async-done(((f32[512,512]{1,0:T(8,128)}), f32[128,512]{1,0:T(8,128)}) %reduce-scatter.3.cloned.1.call-update) | async-done | bytes 262160 | tf_op jit(solution)/shard_map/reduce_scatter | solution.py:50
  103.2 1.7 fusion.19
  104.9 39.5 %all-reduce = (f32[]{:T(128)}, f32[]{:T(128)}) all-reduce(f32[]{:T(128)} %get-tuple-element.106, f32[]{:T(128)} %get-tuple-element.105), channel_id=1, replica_groups=mesh['term'=4,'sector'=8] {'term','sector'}, use_global_device_ids=true, to_apply=%region_5.0 | all-reduce | flops 2 | bytes 16 | tf_op jit(solution)/shard_map/psum | solution.py:57
  145.7 0.0 copy-done
  145.7 1.7 fusion.22
  147.5 41.3 %psum.23 = f32[]{:T(128)} all-reduce(f32[]{:T(128)} %fusion.22), channel_id=1, replica_groups=mesh['term'=4,'sector'=8] {'term','sector'}, use_global_device_ids=true, to_apply=%region_9.0 | all-reduce | flops 1 | bytes 8 | tf_op jit(solution)/shard_map/psum | solution.py:62
  190.1 1.8 fusion.23
  191.9 0.0 all-gather.2.cloned.1.call-update
  192.0 0.0 reduce-scatter.5.cloned.1.call-start
  192.0 26.5 %all-gather.2.cloned.1.call-done = f32[512,512]{1,0:T(8,128)} async-done(((f32[128,512]{1,0:T(8,128)}), f32[512,512]{1,0:T(8,128)}) %all-gather.2.cloned.1.call-update) | async-done | bytes 1048592 | tf_op jit(solution)/shard_map/all_gather | solution.py:64
  218.6 0.4 broadcast.48
  218.9 11.4 %while.23 = (s32[]{:T(128)}, f32[512,3,512]{2,0,1:T(8,128)S(1)}, s32[]{:T(128)}, s32[4]{0:T(128)S(1)}, f32[4,512,512]{2,1,0:T(8,128)}, /*index=5*/f32[512,512]{1...) while((s32[]{:T(128)}, f32[512,3,512]{2,0,1:T(8,128)S(1)}, ...), condition=%wide.region_12.0_spmd, body=%wide.region_10.0_spmd.sunk | while | flops 3221749760 | bytes 7341298 | solution.py:28
  219.6 0.6 dynamic_slice.56
  221.9 0.7 and_reduce_fusion.5
  222.6 3.4 %fusion.50 = f32[512,512]{1,0:T(8,128)S(1)} fusion(f32[512,512]{1,0:T(8,128)} %get-tuple-element.299, f32[4,512,512]{2,1,0:T(8,128)} %get-tuple-element.298, s32[]{:T(128)S(6)} %select_n.30), kind=kOutput, calls=%fused_computation.15.clone.1 | convolution fusion | flops 1610612736 | bytes 3145732 | tf_op jit(solution)/shard_map/while/body/dot_general | solution.py:14
  226.0 3.7 %fusion.51 = f32[512,3,512]{2,0,1:T(8,128)S(1)} fusion(f32[512,3,512]{2,0,1:T(8,128)S(1)} %get-tuple-element.282, s32[]{:T(128)} %select_n.31, f32[512,512]{1,0:T(8,128)S(1)} %fusion.50, f32[4,512,512]{2,1,0:T(8,128)} %get-tuple-element.300, s32[]{:T(128)S(6)} %select_n.30, pred[]{:T(512)} %and_reduce_fusion.5), kind=kOutput, calls=%fused_computation.13.clone.1 | convolution fusion | flops 1611137024 | bytes 4195332 | tf_op jit(solution)/shard_map/while/body/dot_general | solution.py:14
  230.3 0.2 slice_bitcast_fusion.1
  230.5 1.6 collective-permute-start.2
  232.2 1.3 collective-permute-start.3
  233.5 0.9 collective-permute-done.2
  234.4 3.7 %collective-permute-done.3 = f32[512,512]{1,0:T(8,128)S(1)} collective-permute-done((f32[512,512]{1,0:T(8,128)S(1)}, f32[512,512]{1,0:T(8,128)S(1)}, u32[]{:S(2)}, u32[]{:S(2)}) %collective-permute-start.3) | collective-permute-done | bytes 1048608 | tf_op jit(solution)/shard_map/ppermute | solution.py:10
  238.1 1.4 fusion.16
  239.5 0.0 reduce-scatter.5.cloned.1.call-update
  239.5 70.2 %reduce-scatter.5.cloned.1.call-done = f32[128,512]{1,0:T(8,128)} async-done(((f32[512,512]{1,0:T(8,128)}), f32[128,512]{1,0:T(8,128)}) %reduce-scatter.5.cloned.1.call-update) | async-done | bytes 262160 | tf_op jit(solution)/shard_map/reduce_scatter | solution.py:50
Async XLA Ops:
  7.2 1.1 copy-start.1
  7.2 96.0 %reduce-scatter.3.cloned.1.call-start = ((), (), s32[]{:S(2)}) async-start(), calls=%async_computation.2 | async-start | bytes 1310720 | tf_op jit(solution)/shard_map/reduce_scatter | solution.py:50
  20.2 125.5 %copy-start = (f32[1,128,512]{2,1,0:T(8,128)S(1)}, f32[1,128,512]{2,1,0:T(8,128)}, u32[]{:S(2)}) copy-start(f32[1,128,512]{2,1,0:T(8,128)} %param.15) | copy-start | bytes 786436
  20.2 4.8 %collective-permute-start = (f32[512,512]{1,0:T(8,128)S(1)}, f32[512,512]{1,0:T(8,128)S(1)}, u32[]{:S(2)}, u32[]{:S(2)}) collective-permute-start(f32[512,512]{1,0:T(8,128)S(1)} %get-tuple-element.139), channel_id=1, source_target_pairs={{0,1},{1,2},{2,3},{3,4},{4,5},{5,6},{6,7},{8,9},{9,10},{10,11},{11... | collective-permute-start | bytes 3145736 | tf_op jit(solution)/shard_map/ppermute | solution.py:10
  22.8 6.7 %collective-permute-start.1 = (f32[512,512]{1,0:T(8,128)S(1)}, f32[512,512]{1,0:T(8,128)S(1)}, u32[]{:S(2)}, u32[]{:S(2)}) collective-permute-start(f32[512,512]{1,0:T(8,128)S(1)} %get-tuple-element.140), channel_id=1, source_target_pairs={{1,0},{2,1},{3,2},{4,3},{5,4},{6,5},{7,6},{9,8},{10,9},{11,10},{12... | collective-permute-start | bytes 3145736 | tf_op jit(solution)/shard_map/ppermute | solution.py:10
  30.9 187.7 %all-gather.2.cloned.1.call-start = ((), (), s32[]{:S(2)}) async-start(), calls=%async_computation.3 | async-start | bytes 1310720 | tf_op jit(solution)/shard_map/all_gather | solution.py:64
  192.0 117.7 %reduce-scatter.5.cloned.1.call-start = ((), (), s32[]{:S(2)}) async-start(), calls=%async_computation.4 | async-start | bytes 1310720 | tf_op jit(solution)/shard_map/reduce_scatter | solution.py:50
  230.5 3.8 %collective-permute-start.2 = (f32[512,512]{1,0:T(8,128)S(1)}, f32[512,512]{1,0:T(8,128)S(1)}, u32[]{:S(2)}, u32[]{:S(2)}) collective-permute-start(f32[512,512]{1,0:T(8,128)S(1)} %get-tuple-element.137), channel_id=1, source_target_pairs={{0,1},{1,2},{2,3},{3,4},{4,5},{5,6},{6,7},{8,9},{9,10},{10,11},{11... | collective-permute-start | bytes 3145736 | tf_op jit(solution)/shard_map/ppermute | solution.py:10
  232.2 5.9 %collective-permute-start.3 = (f32[512,512]{1,0:T(8,128)S(1)}, f32[512,512]{1,0:T(8,128)S(1)}, u32[]{:S(2)}, u32[]{:S(2)}) collective-permute-start(f32[512,512]{1,0:T(8,128)S(1)} %get-tuple-element.138), channel_id=1, source_target_pairs={{1,0},{2,1},{3,2},{4,3},{5,4},{6,5},{7,6},{9,8},{10,9},{11,10},{12... | collective-permute-start | bytes 3145736 | tf_op jit(solution)/shard_map/ppermute | solution.py:10
Sparse Core Ops, SparseCore 0:
  31.0 72.1 reduce-scatter.2
  192.1 26.4 all-gather.1
  239.6 69.9 reduce-scatter.4
where the time goes:
time: 318 us; the launch traced here: 316 us
  waiting for transfers between devices  179 us (56%)
  blocking collectives  80.9 us (25%)
  between operations  16.5 us (5%)
  matrix products  14.2 us (4%)
  other arithmetic  10 us (3%)
  starting transfers between devices  6.94 us (2%)
  loops' own time  6.29 us (2%)
    reduce_scatter x2, waiting for transfers between devices, apply_hamiltonian(): lax.psum_scatter(whole[:, 1] + upward + downward, 'term', scatter_dimensi...  142 us
    psum x1, blocking collectives, per_device(): correlation_sum = lax.psum(jnp.sum(own_rows * raw), ('term', 'sector'))  41.3 us
    psum x1, blocking collectives, per_device(): lax.psum((jnp.sum(own_rows * first_image), jnp.sum(own_rows * own_rows)),...  39.5 us
    all_gather x1, waiting for transfers between devices, per_device(): full_correction = lax.all_gather(correction, 'term', axis=0, tiled=True)  26.5 us
    dot_general x4, matrix products, matmul(): jnp.dot(first_op, second_op, precision=lax.Precision.HIGHEST, preferred_e...  14.2 us
    ppermute x4, waiting for transfers between devices, from_behind(): return lax.ppermute(block, axis, route)  10 us
    ppermute x4, starting transfers between devices, from_behind(): return lax.ppermute(block, axis, route)  6.82 us
  transfers between devices with their start and end apart: 7, of which 7 were waited for; matrix products, arithmetic and copies ran while one was open for 0% of the time, Pallas kernels for 0%

commit v1 on v0

--- a/solution.py
+++ b/solution.py
@@ -55,7 +55,7 @@
     own_rows = lax.dynamic_slice_in_dim(center, first_own, slab_rows, 0)
     scaling = precond[0]
     cross, norm_sq = lax.psum(
-        (jnp.sum(own_rows * first_image), jnp.sum(own_rows * own_rows)), ("term", "sector")
+        lax.psum((jnp.sum(own_rows * first_image), jnp.sum(own_rows * own_rows)), "sector"), "term"
     )
     rayleigh = cross / norm_sq
     raw = scaling * (first_image - rayleigh * own_rows)

time: 318 us -> 302 us (0.950)
  blocking collectives: 80.9 us -> 63.3 us
    psum x1, blocking collectives: 39.5 us -> 16.8 us  [per_device(): lax.psum((jnp.sum(own_rows * first_image), jnp.sum(own_rows * own_rows)),...]
    psum x0 -> x1, blocking collectives: none -> 9.55 us  [per_device(): lax.psum(lax.psum((jnp.sum(own_rows * first_image), jnp.sum(own_rows * ow...]
    psum x1, blocking collectives: 41.3 us -> 37 us  [per_device(): correlation_sum = lax.psum(jnp.sum(own_rows * raw), ('term', 'sector'))]
where the time goes in v1:
time: 302 us; the launch traced here: 300 us
  waiting for transfers between devices  181 us (60%)
  blocking collectives  63.3 us (21%)
  between operations  16.5 us (5%)
  matrix products  14.2 us (5%)
  other arithmetic  10 us (3%)
  starting transfers between devices  6.94 us (2%)
  loops' own time  6.29 us (2%)
    reduce_scatter x2, waiting for transfers between devices, apply_hamiltonian(): lax.psum_scatter(whole[:, 1] + upward + downward, 'term', scatter_dimensi...  142 us
    psum x1, blocking collectives, per_device(): correlation_sum = lax.psum(jnp.sum(own_rows * raw), ('term', 'sector'))  37 us
    all_gather x1, waiting for transfers between devices, per_device(): full_correction = lax.all_gather(correction, 'term', axis=0, tiled=True)  28.1 us
    psum x1, blocking collectives, per_device(): lax.psum((jnp.sum(own_rows * first_image), jnp.sum(own_rows * own_rows)),...  16.8 us
    dot_general x4, matrix products, matmul(): jnp.dot(first_op, second_op, precision=lax.Precision.HIGHEST, preferred_e...  14.2 us
    ppermute x4, waiting for transfers between devices, from_behind(): return lax.ppermute(block, axis, route)  9.99 us
    psum x1, blocking collectives, per_device(): lax.psum(lax.psum((jnp.sum(own_rows * first_image), jnp.sum(own_rows * ow...  9.55 us
    ppermute x4, starting transfers between devices, from_behind(): return lax.ppermute(block, axis, route)  6.82 us
  transfers between devices with their start and end apart: 7, of which 7 were waited for; matrix products, arithmetic and copies ran while one was open for 0% of the time, Pallas kernels for 0%

profile of v1, /device:TPU:0, one launch (start us, length us, event | category | flops | bytes accessed | tf_op | source)
XLA Modules:
  0.0 300.2 jit_solution(5773341315803560178)
XLA Ops:
  7.2 0.0 copy-start.1
  7.2 0.0 reduce-scatter.3.cloned.1.call-start
  7.2 0.7 add_bitcast_fusion
  7.9 0.4 broadcast.48.clone
  8.3 0.0 copy-done.1
  8.3 11.7 %while.22 = (s32[]{:T(128)}, f32[512,3,512]{2,0,1:T(8,128)S(1)}, s32[]{:T(128)}, s32[4]{0:T(128)S(1)}, f32[4,512,512]{2,1,0:T(8,128)}, /*index=5*/f32[512,512]{1...) while((s32[]{:T(128)}, f32[512,3,512]{2,0,1:T(8,128)S(1)}, ...), condition=%wide.region_2.0_spmd, body=%wide.region_0.0_spmd.sunk | while | flops 3221749760 | bytes 7341298 | solution.py:28
  9.0 0.6 dynamic_slice.53
  11.5 0.7 and_reduce_fusion.4
  12.2 3.4 %fusion.44 = f32[512,512]{1,0:T(8,128)S(1)} fusion(f32[512,512]{1,0:T(8,128)} %get-tuple-element.262, f32[4,512,512]{2,1,0:T(8,128)} %get-tuple-element.261, s32[]{:T(128)S(6)} %select_n.28), kind=kOutput, calls=%fused_computation.4.clone.1 | convolution fusion | flops 1610612736 | bytes 3145732 | tf_op jit(solution)/shard_map/while/body/dot_general | solution.py:14
  15.6 3.8 %fusion.45 = f32[512,3,512]{2,0,1:T(8,128)S(1)} fusion(f32[512,3,512]{2,0,1:T(8,128)S(1)} %get-tuple-element.245, s32[]{:T(128)} %select_n.29, f32[512,512]{1,0:T(8,128)S(1)} %fusion.44, f32[4,512,512]{2,1,0:T(8,128)} %get-tuple-element.263, s32[]{:T(128)S(6)} %select_n.28, pred[]{:T(512)} %and_reduce_fusion.4), kind=kOutput, calls=%fused_computation.2.clone.1 | convolution fusion | flops 1611137024 | bytes 4195332 | tf_op jit(solution)/shard_map/while/body/dot_general | solution.py:14
  20.0 0.2 slice_bitcast_fusion.3
  20.2 0.0 copy-start
  20.2 2.6 collective-permute-start
  22.8 1.3 collective-permute-start.1
  24.1 0.9 collective-permute-done
  25.0 4.5 %collective-permute-done.1 = f32[512,512]{1,0:T(8,128)S(1)} collective-permute-done((f32[512,512]{1,0:T(8,128)S(1)}, f32[512,512]{1,0:T(8,128)S(1)}, u32[]{:S(2)}, u32[]{:S(2)}) %collective-permute-start.1) | collective-permute-done | bytes 1048608 | tf_op jit(solution)/shard_map/ppermute | solution.py:10
  29.5 1.4 fusion.17
  30.9 0.0 reduce-scatter.3.cloned.1.call-update
  30.9 0.0 all-gather.2.cloned.1.call-start
  30.9 72.2 %reduce-scatter.3.cloned.1.call-done = f32[128,512]{1,0:T(8,128)} async-done(((f32[512,512]{1,0:T(8,128)}), f32[128,512]{1,0:T(8,128)}) %reduce-scatter.3.cloned.1.call-update) | async-done | bytes 262160 | tf_op jit(solution)/shard_map/reduce_scatter | solution.py:50
  103.2 1.7 fusion.19
  104.9 16.8 %all-reduce = (f32[]{:T(128)}, f32[]{:T(128)}) all-reduce(f32[]{:T(128)} %get-tuple-element.106, f32[]{:T(128)} %get-tuple-element.105), channel_id=1, replica_groups=mesh['term'=4,'sector'=8] {'sector'}, use_global_device_ids=true, to_apply=%region_5.0 | all-reduce | flops 2 | bytes 16 | tf_op jit(solution)/shard_map/psum | solution.py:58
  121.7 9.6 %all-reduce.1 = (f32[]{:T(128)}, f32[]{:T(128)}) all-reduce(f32[]{:T(128)} %get-tuple-element.135, f32[]{:T(128)} %get-tuple-element.136), channel_id=1, replica_groups=mesh['term'=4,'sector'=8] {'term'}, use_global_device_ids=true, to_apply=%region_6.0 | all-reduce | flops 2 | bytes 16 | tf_op jit(solution)/shard_map/psum | solution.py:57
  132.6 0.0 copy-done
  132.6 1.7 fusion.22
  134.3 37.0 %psum.39 = f32[]{:T(128)} all-reduce(f32[]{:T(128)} %fusion.22), channel_id=1, replica_groups=mesh['term'=4,'sector'=8] {'term','sector'}, use_global_device_ids=true, to_apply=%region_11.0 | all-reduce | flops 1 | bytes 8 | tf_op jit(solution)/shard_map/psum | solution.py:62
  172.6 1.8 fusion.23
  174.4 0.0 all-gather.2.cloned.1.call-update
  174.5 0.0 reduce-scatter.5.cloned.1.call-start
  174.5 28.1 %all-gather.2.cloned.1.call-done = f32[512,512]{1,0:T(8,128)} async-done(((f32[128,512]{1,0:T(8,128)}), f32[512,512]{1,0:T(8,128)}) %all-gather.2.cloned.1.call-update) | async-done | bytes 1048592 | tf_op jit(solution)/shard_map/all_gather | solution.py:64
  202.6 0.4 broadcast.48
  203.0 11.4 %while.23 = (s32[]{:T(128)}, f32[512,3,512]{2,0,1:T(8,128)S(1)}, s32[]{:T(128)}, s32[4]{0:T(128)S(1)}, f32[4,512,512]{2,1,0:T(8,128)}, /*index=5*/f32[512,512]{1...) while((s32[]{:T(128)}, f32[512,3,512]{2,0,1:T(8,128)S(1)}, ...), condition=%wide.region_14.0_spmd, body=%wide.region_12.0_spmd.sunk | while | flops 3221749760 | bytes 7341298 | solution.py:28
  203.7 0.6 dynamic_slice.56
  206.0 0.7 and_reduce_fusion.5
  206.7 3.4 %fusion.50 = f32[512,512]{1,0:T(8,128)S(1)} fusion(f32[512,512]{1,0:T(8,128)} %get-tuple-element.301, f32[4,512,512]{2,1,0:T(8,128)} %get-tuple-element.300, s32[]{:T(128)S(6)} %select_n.30), kind=kOutput, calls=%fused_computation.15.clone.1 | convolution fusion | flops 1610612736 | bytes 3145732 | tf_op jit(solution)/shard_map/while/body/dot_general | solution.py:14
  210.1 3.7 %fusion.51 = f32[512,3,512]{2,0,1:T(8,128)S(1)} fusion(f32[512,3,512]{2,0,1:T(8,128)S(1)} %get-tuple-element.284, s32[]{:T(128)} %select_n.31, f32[512,512]{1,0:T(8,128)S(1)} %fusion.50, f32[4,512,512]{2,1,0:T(8,128)} %get-tuple-element.302, s32[]{:T(128)S(6)} %select_n.30, pred[]{:T(512)} %and_reduce_fusion.5), kind=kOutput, calls=%fused_computation.13.clone.1 | convolution fusion | flops 1611137024 | bytes 4195332 | tf_op jit(solution)/shard_map/while/body/dot_general | solution.py:14
  214.4 0.2 slice_bitcast_fusion.1
  214.6 1.6 collective-permute-start.2
  216.2 1.3 collective-permute-start.3
  217.5 0.9 collective-permute-done.2
  218.5 3.7 %collective-permute-done.3 = f32[512,512]{1,0:T(8,128)S(1)} collective-permute-done((f32[512,512]{1,0:T(8,128)S(1)}, f32[512,512]{1,0:T(8,128)S(1)}, u32[]{:S(2)}, u32[]{:S(2)}) %collective-permute-start.3) | collective-permute-done | bytes 1048608 | tf_op jit(solution)/shard_map/ppermute | solution.py:10
  222.2 1.4 fusion.16
  223.5 0.0 reduce-scatter.5.cloned.1.call-update
  223.6 70.2 %reduce-scatter.5.cloned.1.call-done = f32[128,512]{1,0:T(8,128)} async-done(((f32[512,512]{1,0:T(8,128)}), f32[128,512]{1,0:T(8,128)}) %reduce-scatter.5.cloned.1.call-update) | async-done | bytes 262160 | tf_op jit(solution)/shard_map/reduce_scatter | solution.py:50
Async XLA Ops:
  7.2 1.1 copy-start.1
  7.2 96.0 %reduce-scatter.3.cloned.1.call-start = ((), (), s32[]{:S(2)}) async-start(), calls=%async_computation.2 | async-start | bytes 1310720 | tf_op jit(solution)/shard_map/reduce_scatter | solution.py:50
  20.2 112.3 %copy-start = (f32[1,128,512]{2,1,0:T(8,128)S(1)}, f32[1,128,512]{2,1,0:T(8,128)}, u32[]{:S(2)}) copy-start(f32[1,128,512]{2,1,0:T(8,128)} %param.15) | copy-start | bytes 786436
  20.2 4.8 %collective-permute-start = (f32[512,512]{1,0:T(8,128)S(1)}, f32[512,512]{1,0:T(8,128)S(1)}, u32[]{:S(2)}, u32[]{:S(2)}) collective-permute-start(f32[512,512]{1,0:T(8,128)S(1)} %get-tuple-element.141), channel_id=1, source_target_pairs={{0,1},{1,2},{2,3},{3,4},{4,5},{5,6},{6,7},{8,9},{9,10},{10,11},{11... | collective-permute-start | bytes 3145736 | tf_op jit(solution)/shard_map/ppermute | solution.py:10
  22.8 6.7 %collective-permute-start.1 = (f32[512,512]{1,0:T(8,128)S(1)}, f32[512,512]{1,0:T(8,128)S(1)}, u32[]{:S(2)}, u32[]{:S(2)}) collective-permute-start(f32[512,512]{1,0:T(8,128)S(1)} %get-tuple-element.142), channel_id=1, source_target_pairs={{1,0},{2,1},{3,2},{4,3},{5,4},{6,5},{7,6},{9,8},{10,9},{11,10},{12... | collective-permute-start | bytes 3145736 | tf_op jit(solution)/shard_map/ppermute | solution.py:10
  30.9 171.7 %all-gather.2.cloned.1.call-start = ((), (), s32[]{:S(2)}) async-start(), calls=%async_computation.3 | async-start | bytes 1310720 | tf_op jit(solution)/shard_map/all_gather | solution.py:64
  174.5 119.3 %reduce-scatter.5.cloned.1.call-start = ((), (), s32[]{:S(2)}) async-start(), calls=%async_computation.4 | async-start | bytes 1310720 | tf_op jit(solution)/shard_map/reduce_scatter | solution.py:50
  214.6 3.9 %collective-permute-start.2 = (f32[512,512]{1,0:T(8,128)S(1)}, f32[512,512]{1,0:T(8,128)S(1)}, u32[]{:S(2)}, u32[]{:S(2)}) collective-permute-start(f32[512,512]{1,0:T(8,128)S(1)} %get-tuple-element.139), channel_id=1, source_target_pairs={{0,1},{1,2},{2,3},{3,4},{4,5},{5,6},{6,7},{8,9},{9,10},{10,11},{11... | collective-permute-start | bytes 3145736 | tf_op jit(solution)/shard_map/ppermute | solution.py:10
  216.2 5.9 %collective-permute-start.3 = (f32[512,512]{1,0:T(8,128)S(1)}, f32[512,512]{1,0:T(8,128)S(1)}, u32[]{:S(2)}, u32[]{:S(2)}) collective-permute-start(f32[512,512]{1,0:T(8,128)S(1)} %get-tuple-element.140), channel_id=1, source_target_pairs={{1,0},{2,1},{3,2},{4,3},{5,4},{6,5},{7,6},{9,8},{10,9},{11,10},{12... | collective-permute-start | bytes 3145736 | tf_op jit(solution)/shard_map/ppermute | solution.py:10
Sparse Core Ops, SparseCore 0:
  31.0 72.1 reduce-scatter.2
  174.6 28.0 all-gather.1
  223.7 69.9 reduce-scatter.4
